TPU v7x, 32 devices: a whole 2x2x4 slice. The times are simulated.
32 devices in a mesh: dp: 4 (over x, y), ep: 8 (over z, core).
Axes of the slice: x: 2, y: 2, z: 4, core: 2. Of those that a mesh axis runs over, the one named last changes fastest.
Arguments:
- x: bfloat16 [4, 8, 256, 4096], P('dp', 'ep'), parts along dimension 0
- expert: int32 [4, 8, 256, 2], P('dp', 'ep'), parts along dimension 0
- slot: int32 [4, 8, 256, 2], P('dp', 'ep'), parts along dimension 0
- gate: float32 [4, 8, 256, 2], P('dp', 'ep'), parts along dimension 0
- w_gate: bfloat16 [16, 4096, 6400], P('ep')
- w_up: bfloat16 [16, 4096, 6400], P('ep')
- w_down: bfloat16 [16, 6400, 4096], P('ep')
Outputs:
- y: bfloat16 [4, 8, 256, 4096], P('dp', 'ep'), parts along dimension 0
There are 4 independent parts. A program takes and returns all parts, laid end to end along the dimension named above; an argument that names none is the same for every part.
All inputs are finite; a program needn't handle non-finite values.
Results may differ from a plain program's by a relative error of at most 0.009.
Values are sent between devices in bfloat16 or wider.
A program may use at most 2 GiB of HBM per device.

v0:
```python
import jax
import jax.numpy as jnp
from jax import lax
from jax.sharding import NamedSharding, PartitionSpec as P


def einsum(form, a, b):
    return jnp.einsum(form, a.astype(jnp.float32), b.astype(jnp.float32))


def solution(mesh):
    def placed(v, *spec):
        return lax.with_sharding_constraint(v, NamedSharding(mesh, P(*spec)))

    def step(x, expert, slot, gate, w_gate, w_up, w_down):
        experts, (tokens, top) = w_gate.shape[0], expert.shape[2:]
        slots = 5 * tokens * top // (4 * experts)
        to_expert = jax.nn.one_hot(expert, experts, dtype=jnp.bfloat16)
        to_slot = jax.nn.one_hot(slot, slots, dtype=jnp.bfloat16)
        weighted = to_expert * gate[..., None].astype(jnp.bfloat16)
        dispatch = einsum("abtke,abtkc->abtec", to_expert, to_slot).astype(jnp.bfloat16)
        combine = einsum("abtke,abtkc->abtec", weighted, to_slot).astype(jnp.bfloat16)
        z = einsum("abtec,abtd->aebcd", dispatch, x).astype(jnp.bfloat16)
        z = placed(z, "dp", None, "ep", None, None)
        z = placed(z, "dp", "ep", None, None, None)
        h = jax.nn.silu(einsum("aebcd,edf->aebcf", z, w_gate))
        h = (h * einsum("aebcd,edf->aebcf", z, w_up)).astype(jnp.bfloat16)
        out = einsum("aebcf,efd->aebcd", h, w_down).astype(jnp.bfloat16)
        out = placed(out, "dp", "ep", None, None, None)
        out = placed(out, "dp", None, "ep", None, None)
        y = einsum("abtec,aebcd->abtd", combine, out)
        return y.astype(jnp.bfloat16)

    return step
```

profile of v0, /device:TPU:0, one launch (start us, length us, event | category | flops | bytes accessed | tf_op | source)
XLA Modules:
  0.0 407.3 jit_solution(10236897648071596871)
XLA Ops:
  0.0 0.0 copy-start
  0.0 1.0 copy.11
  1.0 0.0 copy-start.1
  1.0 0.8 copy.9
  1.8 0.0 copy-start.3
  1.8 2.0 convolution_convert_fusion.1
  3.8 0.0 copy-done
  3.9 1.7 convolution_convert_fusion
  5.6 122.7 %all-to-all.4 = bf16[1,8,2,1,40,4096]{5,4,2,3,0,1:T(8,128)(2,1)} all-to-all(bf16[1,8,2,1,40,4096]{5,4,2,3,0,1:T(8,128)(2,1)S(1)} %bitcast.93), channel_id=1, replica_groups=mesh['dp'=4,'ep'=8] {'ep'}, dimensions={1} | all-to-all | bytes 10485760 | tf_op jit(solution)/sharding_constraint;jit(solution)/sharding_constraint | solution.py:13
  128.2 0.0 copy-done.1
  128.2 0.0 copy-done.3
  128.3 48.3 %fusion.4 = f32[2,8,40,6400]{3,2,1,0:T(8,128)} fusion(bf16[2,4096,6400]{2,1,0:T(8,128)(2,1)} %param.4, bf16[1,8,2,1,40,4096]{5,4,2,3,0,1:T(8,128)(2,1)} %all-to-all.4), kind=kOutput, calls=%fused_computation.4 | convolution fusion | flops 33554432000 | bytes 126484480 | tf_op jit(solution)/aebcd,edf->aebcf/dot_general | solution.py:8
  176.6 49.7 %fusion.12 = bf16[2,8,40,6400]{3,2,1,0:T(8,128)(2,1)} fusion(bf16[2,4096,6400]{2,1,0:T(8,128)(2,1)} %param.5, f32[2,8,40,6400]{3,2,1,0:T(8,128)} %fusion.4, bf16[1,8,2,1,40,4096]{5,4,2,3,0,1:T(8,128)(2,1)} %all-to-all.4), kind=kOutput, calls=%fused_computation.13 | convolution fusion | flops 33579008000 | bytes 134676480 | tf_op jit(solution)/aebcd,edf->aebcf/dot_general | solution.py:8
  226.3 49.0 %fusion.18 = bf16[1,2,8,1,40,4096]{5,4,2,1,3,0:T(8,128)(2,1)} fusion(bf16[2,8,40,6400]{3,2,1,0:T(8,128)(2,1)} %fusion.12, bf16[2,6400,4096]{2,1,0:T(8,128)(2,1)} %param.6), kind=kOutput, calls=%fused_computation.16 | convolution fusion | flops 33557053440 | bytes 118292480 | tf_op jit(solution)/aebcf,efd->aebcd/dot_general | solution.py:8
  275.2 0.0 copy-start.5
  275.3 5.5 %copy.15 = bf16[1,2,8,1,40,4096]{5,4,1,3,0,2:T(8,128)(2,1)} copy(bf16[1,2,8,1,40,4096]{5,4,2,1,3,0:T(8,128)(2,1)} %fusion.18) | data formatting | bytes 10485760 | tf_op jit(solution)/sharding_constraint;jit(solution)/sharding_constraint | solution.py:13
  280.7 4.7 %all-to-all-start.1 = ((bf16[1,2,8,1,40,4096]{5,4,1,3,0,2:T(8,128)(2,1)}), bf16[1,2,8,1,40,4096]{5,4,1,3,0,2:T(8,128)(2,1)}, u32[]{:S(2)}, u32[]{:S(2)}) async-start(bf16[1,2,8,1,40,4096]{5,4,1,3,0,2:T(8,128)(2,1)} %copy.15), calls=%async_computation.1 | async-start | bytes 10485760 | tf_op jit(solution)/sharding_constraint;jit(solution)/sharding_constraint | solution.py:13
  285.4 0.0 copy-done.5
  285.4 0.1 copy.10
  285.6 0.0 copy-done.2
  285.6 0.0 copy-done.4
  285.6 2.4 convolution_convert_fusion.2
  288.0 113.5 %all-to-all-done.1 = bf16[1,2,8,1,40,4096]{5,4,1,3,0,2:T(8,128)(2,1)} async-done(((bf16[1,2,8,1,40,4096]{5,4,1,3,0,2:T(8,128)(2,1)}), bf16[1,2,8,1,40,4096]{5,4,1,3,0,2:T(8,128)(2,1)}, u32[]{:S(2)}, u32[]{:S(2)}) %all-to-all-start.1) | async-done | bytes 5242912 | tf_op jit(solution)/sharding_constraint;jit(solution)/sharding_constraint | solution.py:13
  401.6 5.8 %fusion.24 = bf16[1,1,256,4096]{3,2,1,0:T(8,128)(2,1)} fusion(bf16[16,40,4096]{2,1,0:T(8,128)(2,1)} %bitcast.25, bf16[256,16,40]{2,1,0:T(8,128)(2,1)S(1)} %convolution_convert_fusion.2), kind=kOutput, calls=%fused_computation.21 | convolution fusion | flops 1343225856 | bytes 7667712 | tf_op jit(solution)/abtec,aebcd->abtd/dot_general | solution.py:8
  (3 shorter events, 0.0 us)
Async XLA Ops:
  0.0 3.8 copy-start
  1.0 127.3 %copy-start.1 = (s32[256,2]{1,0:T(8,128)}, s32[256,2]{1,0:T(8,128)S(1)}, u32[]{:S(2)}) copy-start(s32[256,2]{1,0:T(8,128)S(1)} %copy.11) | copy-start | bytes 6148
  1.8 126.4 %copy-start.3 = (s32[256,2]{1,0:T(8,128)}, s32[256,2]{1,0:T(8,128)S(1)}, u32[]{:S(2)}) copy-start(s32[256,2]{1,0:T(8,128)S(1)} %copy.9) | copy-start | bytes 6148
  275.2 10.2 %copy-start.5 = (f32[1,1,256,2]{2,3,1,0:T(2,128)S(1)}, f32[1,1,256,2]{2,3,1,0:T(2,128)}, u32[]{:S(2)}) copy-start(f32[1,1,256,2]{2,3,1,0:T(2,128)} %param.1) | copy-start | bytes 6148
  275.2 10.3 %copy-start.2 = (s32[256,2]{1,0:T(8,128)S(1)}, s32[256,2]{1,0:T(8,128)}, u32[]{:S(2)}) copy-start(s32[256,2]{1,0:T(8,128)} %copy-done.1) | copy-start | bytes 6148
  275.2 10.3 %copy-start.4 = (s32[256,2]{1,0:T(8,128)S(1)}, s32[256,2]{1,0:T(8,128)}, u32[]{:S(2)}) copy-start(s32[256,2]{1,0:T(8,128)} %copy-done.3) | copy-start | bytes 6148
  280.7 120.8 %all-to-all-start.1 = ((bf16[1,2,8,1,40,4096]{5,4,1,3,0,2:T(8,128)(2,1)}), bf16[1,2,8,1,40,4096]{5,4,1,3,0,2:T(8,128)(2,1)}, u32[]{:S(2)}, u32[]{:S(2)}) async-start(bf16[1,2,8,1,40,4096]{5,4,1,3,0,2:T(8,128)(2,1)} %copy.15), calls=%async_computation.1 | async-start | bytes 10485760 | tf_op jit(solution)/sharding_constraint;jit(solution)/sharding_constraint | solution.py:13
where the time goes:
time: 408 us; the launch traced here: 407 us
  matrix products  159 us (39%)
  blocking collectives  123 us (30%)
  waiting for transfers between devices  114 us (28%)
  local copies, waits for them, and re-layouts  7.44 us (2%)
  starting transfers between devices  4.68 us (1%)
    dot_general x7, matrix products, einsum(): return jnp.einsum(form, a.astype(jnp.float32), b.astype(jnp.float32))  159 us
    another operation x1, blocking collectives, placed(): return lax.with_sharding_constraint(v, NamedSharding(mesh, P(*spec)))  123 us
    another operation x1, waiting for transfers between devices, placed(): return lax.with_sharding_constraint(v, NamedSharding(mesh, P(*spec)))  114 us
  transfers between devices with their start and end apart: 1, of which 1 were waited for; matrix products, arithmetic and copies ran while one was open for 1% of the time, Pallas kernels for 0%

commit v1 on v0

v1 whole, which is shorter than its diff:
```python
import functools

import jax
import jax.numpy as jnp
from jax import lax
from jax.experimental import pallas as pl
from jax.experimental.pallas import tpu as pltpu
from jax.sharding import PartitionSpec as P

TILE = 256
STEPS_IN, STEPS_OUT = 5, 4


def ffn_kernel(z_hbm, w_gate, w_up, w_down, o_hbm, pool, z, h, stage, sem, z_sem, o_sem, *, k):
    rows, d = z.shape
    ff = h.shape[1]
    wide, deep = ff // STEPS_IN, d // STEPS_OUT

    def load_in(t, slot):
        c = pl.ds(pl.multiple_of(t * wide, 128), wide)
        return [
            pltpu.make_async_copy(w_gate.at[k, :, c], pool.at[slot, pl.ds(0, d), :], sem.at[slot, 0]),
            pltpu.make_async_copy(w_up.at[k, :, c], pool.at[slot, pl.ds(d, d), :], sem.at[slot, 1]),
        ]

    def load_first(i):
        c = pl.ds(i * TILE, TILE)
        return [
            pltpu.make_async_copy(w_gate.at[k, :, c], pool.at[0, pl.ds(0, d), c], sem.at[0, 2 * i]),
            pltpu.make_async_copy(w_up.at[k, :, c], pool.at[0, pl.ds(d, d), c], sem.at[0, 2 * i + 1]),
        ]

    def load_out(t, slot):
        c = pl.ds(pl.multiple_of(t * deep, 128), deep)
        return pltpu.make_async_copy(w_down.at[k, :, c], pool.at[slot, pl.ds(0, ff), pl.ds(0, deep)], sem.at[slot, 0])

    def store(t, slot):
        c = pl.ds(pl.multiple_of(t * deep, 128), deep)
        return pltpu.make_async_copy(stage.at[slot], o_hbm.at[:, c], o_sem.at[slot])

    def project_in(t, slot, i):
        c = pl.ds(i * TILE, TILE)
        g = jnp.dot(z[...], pool[slot, pl.ds(0, d), c], preferred_element_type=jnp.float32)
        u = jnp.dot(z[...], pool[slot, pl.ds(d, d), c], preferred_element_type=jnp.float32)
        h[:, pl.ds(pl.multiple_of(t * wide + i * TILE, 128), TILE)] = (g * jax.nn.sigmoid(g) * u).astype(h.dtype)

    tokens = pltpu.make_async_copy(z_hbm, z, z_sem)
    for i in range(wide // TILE):
        for copy in load_first(i):
            copy.start()
        if i == 0:
            tokens.start()

    for i in range(wide // TILE):
        for copy in load_first(i):
            copy.wait()
        if i == 0:
            tokens.wait()
            for copy in load_in(1, 1):
                copy.start()
        project_in(0, 0, i)

    @pl.loop(1, STEPS_IN)
    def _(t):
        slot = lax.rem(t, 2)
        for copy in load_in(t, slot):
            copy.wait()

        @pl.when(t + 1 < STEPS_IN)
        def _():
            for copy in load_in(t + 1, 1 - slot):
                copy.start()

        @pl.when(t + 1 == STEPS_IN)
        def _():
            load_out(0, 1 - slot).start()

        for i in range(wide // TILE):
            project_in(t, slot, i)

    @pl.loop(0, STEPS_OUT)
    def _(t):
        slot, mine = lax.rem(t + STEPS_IN, 2), lax.rem(t, 2)
        load_out(t, slot).wait()

        @pl.when(t + 1 < STEPS_OUT)
        def _():
            load_out(t + 1, 1 - slot).start()

        @pl.when(t >= 2)
        def _():
            store(t - 2, mine).wait()

        for i in range(deep // TILE):
            c = pl.ds(i * TILE, TILE)
            out = jnp.dot(h[...], pool[slot, pl.ds(0, ff), c], preferred_element_type=jnp.float32)
            stage[mine, :, c] = out.astype(stage.dtype)
        store(t, mine).start()

    for t in range(STEPS_OUT - 2, STEPS_OUT):
        store(t, t % 2).wait()


def ffn(z, w_gate, w_up, w_down, k):
    (rows, d), ff = z.shape, w_gate.shape[2]
    anywhere = pl.BlockSpec(memory_space=pl.ANY)
    return pl.pallas_call(
        functools.partial(ffn_kernel, k=k),
        in_specs=[anywhere] * 4,
        out_specs=anywhere,
        out_shape=jax.ShapeDtypeStruct((rows, d), jnp.bfloat16),
        scratch_shapes=[
            pltpu.VMEM((2, 2 * d, ff // STEPS_IN), jnp.bfloat16),
            pltpu.VMEM((rows, d), jnp.bfloat16),
            pltpu.VMEM((rows, ff), jnp.bfloat16),
            pltpu.VMEM((2, rows, d // STEPS_OUT), jnp.bfloat16),
            pltpu.SemaphoreType.DMA((2, 2 * ff // STEPS_IN // TILE)),
            pltpu.SemaphoreType.DMA,
            pltpu.SemaphoreType.DMA((2,)),
        ],
        compiler_params=pltpu.CompilerParams(vmem_limit_bytes=60 * 2**20),
        cost_estimate=pl.CostEstimate(flops=6 * rows * d * ff, bytes_accessed=6 * d * ff, transcendentals=0),
        name=f"ffn{k}",
    )(z, w_gate, w_up, w_down)


def solution(mesh):
    devices = mesh.shape["ep"]

    def body(x, expert, slot, gate, w_gate, w_up, w_down):
        x, expert, slot, gate = x[0, 0], expert[0, 0], slot[0, 0], gate[0, 0]
        (tokens, d), top = x.shape, expert.shape[1]
        local = w_gate.shape[0]
        experts = devices * local
        slots = 5 * tokens * top // (4 * experts)
        place = jnp.where(slot < slots, expert * slots + slot, -1)
        weight = gate.astype(jnp.bfloat16)

        def rows_of(k):
            e = jnp.arange(devices, dtype=jnp.int32)[:, None] * local + k
            return (e * slots + jnp.arange(slots, dtype=jnp.int32)).reshape(-1)

        zs = []
        for k in range(local):
            dispatch = jnp.any(rows_of(k)[:, None, None] == place[None], axis=2).astype(jnp.bfloat16)
            sent = jnp.dot(dispatch, x, preferred_element_type=jnp.float32).astype(jnp.bfloat16)
            z = lax.all_to_all(sent.reshape(devices, slots, d), "ep", 0, 0)
            zs.append(z.reshape(devices * slots, d))
        y = 0
        for k in range(local):
            out = ffn(zs[k], w_gate, w_up, w_down, k)
            back = lax.all_to_all(out.reshape(devices, slots, d), "ep", 0, 0)
            hit = rows_of(k)[None, :, None] == place[:, None]
            combine = jnp.sum(jnp.where(hit, weight[:, None], 0), axis=2, dtype=jnp.bfloat16)
            y += jnp.dot(combine, back.reshape(devices * slots, d), preferred_element_type=jnp.float32)
        return y.astype(jnp.bfloat16)[None, None]

    by_token, by_expert = P("dp", "ep", None, None), P("ep", None, None)
    return jax.shard_map(
        body,
        mesh=mesh,
        in_specs=(by_token,) * 4 + (by_expert,) * 3,
        out_specs=by_token,
        check_vma=False,
    )
```

time: 408 us -> 278 us (0.68)
  matrix products: 159 us -> 15.3 us
  Pallas kernels: 0 us -> 126 us
  blocking collectives: 123 us -> 0 us
  starting transfers between devices: 4.68 us -> 20.9 us
  local copies, waits for them, and re-layouts: 7.44 us -> 0.77 us
    dot_general x7 -> x4, matrix products: 159 us -> 15.3 us  [the longest x2 10.5 us: body(): jnp.dot(combine, back.reshape(devices * slots, d), preferred_element_type...]
    pallas_call x0 -> x2, Pallas kernels: none -> 126 us  [ffn(): pl.pallas_call(functools.partial(ffn_kernel, k=k), in_specs=[anywhere] *...]
    another operation x1 -> x0, blocking collectives: 123 us -> none  [placed(): return lax.with_sharding_constraint(v, NamedSharding(mesh, P(*spec)))]
    another operation x1 -> x0, waiting for transfers between devices: 114 us -> none  [placed(): return lax.with_sharding_constraint(v, NamedSharding(mesh, P(*spec)))]
    all_to_all x0 -> x4, waiting for transfers between devices: none -> 113 us  [the longest x2 57.7 us: body(): z = lax.all_to_all(sent.reshape(devices, slots, d), 'ep', 0, 0)]
    all_to_all x0 -> x4, starting transfers between devices: none -> 20.9 us  [the longest x2 10.8 us: body(): z = lax.all_to_all(sent.reshape(devices, slots, d), 'ep', 0, 0)]
    another operation x1 -> x0, local copies, waits for them, and re-layouts: 5.48 us -> none  [placed(): return lax.with_sharding_constraint(v, NamedSharding(mesh, P(*spec)))]
    another operation x1 -> x0, starting transfers between devices: 4.68 us -> none  [placed(): return lax.with_sharding_constraint(v, NamedSharding(mesh, P(*spec)))]
  transfers between devices with their start and end apart: 1 -> 4, of which waited for: 1 -> 2; matrix products, arithmetic and copies ran while one was open for 1% -> 3% of each run, Pallas kernels for 0% -> 45%
where the time goes in v1:
time: 278 us; the launch traced here: 277 us
  Pallas kernels  126 us (45%)
  waiting for transfers between devices  113 us (41%)
  starting transfers between devices  20.9 us (8%)
  matrix products  15.3 us (6%)
    pallas_call x2, Pallas kernels, ffn(): pl.pallas_call(functools.partial(ffn_kernel, k=k), in_specs=[anywhere] *...  126 us
    all_to_all x2, waiting for transfers between devices, body(): z = lax.all_to_all(sent.reshape(devices, slots, d), 'ep', 0, 0)  57.7 us
    all_to_all x2, waiting for transfers between devices, body(): back = lax.all_to_all(out.reshape(devices, slots, d), 'ep', 0, 0)  54.8 us
    all_to_all x2, starting transfers between devices, body(): z = lax.all_to_all(sent.reshape(devices, slots, d), 'ep', 0, 0)  10.8 us
    dot_general x2, matrix products, body(): jnp.dot(combine, back.reshape(devices * slots, d), preferred_element_type...  10.5 us
    all_to_all x2, starting transfers between devices, body(): back = lax.all_to_all(out.reshape(devices, slots, d), 'ep', 0, 0)  10.1 us
  transfers between devices with their start and end apart: 4, of which 2 were waited for; matrix products, arithmetic and copies ran while one was open for 3% of the time, Pallas kernels for 45%

profile of v1, /device:TPU:0, one launch (start us, length us, event | category | flops | bytes accessed | tf_op | source)
XLA Modules:
  0.0 277.1 jit_solution(4858837436025656856)
XLA Ops:
  0.0 0.1 iota_add_fusion
  0.1 0.1 add.113
  0.2 0.1 iota_add_fusion.1
  0.2 0.1 add.107
  0.3 0.9 fusion.6
  1.2 0.6 copy-done.5
  1.8 0.2 compare_reduce_fusion
  2.0 2.4 convolution_convert_fusion.1
  4.4 6.4 %all-to-all-start = ((bf16[8,40,4096]{2,1,0:T(8,128)(2,1)}), bf16[8,40,4096]{2,1,0:T(8,128)(2,1)}, u32[]{:S(2)}, u32[]{:S(2)}) async-start(bf16[8,40,4096]{2,1,0:T(8,128)(2,1)} %bitcast.26), calls=%async_computation | async-start | bytes 5242880 | tf_op jit(solution)/shard_map/all_to_all | solution.py:147
  10.8 2.4 convolution_convert_fusion
  13.1 57.7 %all-to-all-done = bf16[8,40,4096]{2,1,0:T(8,128)(2,1)} async-done(((bf16[8,40,4096]{2,1,0:T(8,128)(2,1)}), bf16[8,40,4096]{2,1,0:T(8,128)(2,1)}, u32[]{:S(2)}, u32[]{:S(2)}) %all-to-all-start) | async-done | bytes 2621472 | tf_op jit(solution)/shard_map/all_to_all | solution.py:147
  70.9 4.4 %all-to-all-start.2 = ((bf16[8,40,4096]{2,1,0:T(8,128)(2,1)}), bf16[8,40,4096]{2,1,0:T(8,128)(2,1)}, u32[]{:S(2)}, u32[]{:S(2)}) async-start(bf16[8,40,4096]{2,1,0:T(8,128)(2,1)} %bitcast.25), calls=%async_computation.2 | async-start | bytes 5242880 | tf_op jit(solution)/shard_map/all_to_all | solution.py:147
  75.3 62.9 %ffn0.1 = bf16[320,4096]{1,0:T(8,128)(2,1)} custom-call(bf16[320,4096]{1,0:T(8,128)(2,1)} %bitcast.4.z_hbm, bf16[2,4096,6400]{2,1,0:T(8,128)(2,1)} %w_gate.3, bf16[2,4096,6400]{2,1,0:T(8,128)(2,1)} %w_up.3, bf16[2,6400,4096]{2,1,0:T(8,128)(2,1)} %w_down.3), custom_call_target="tpu_custom_call" | custom-call | flops 50331648000 | bytes 157286400 | tf_op jit(solution)/shard_map/ffn0/pallas_call | solution.py:107
  138.2 0.0 all-to-all-done.2
  138.2 5.0 %all-to-all-start.1 = ((bf16[8,40,4096]{2,1,0:T(8,128)(2,1)}), bf16[8,40,4096]{2,1,0:T(8,128)(2,1)}, u32[]{:S(2)}, u32[]{:S(2)}) async-start(bf16[8,40,4096]{2,1,0:T(8,128)(2,1)} %bitcast.28), calls=%async_computation.1 | async-start | bytes 5242880 | tf_op jit(solution)/shard_map/all_to_all | solution.py:152
  143.2 63.0 %ffn1.1 = bf16[320,4096]{1,0:T(8,128)(2,1)} custom-call(bf16[320,4096]{1,0:T(8,128)(2,1)} %bitcast.8.z_hbm, bf16[2,4096,6400]{2,1,0:T(8,128)(2,1)} %w_gate.3, bf16[2,4096,6400]{2,1,0:T(8,128)(2,1)} %w_up.3, bf16[2,6400,4096]{2,1,0:T(8,128)(2,1)} %w_down.3), custom_call_target="tpu_custom_call" | custom-call | flops 50331648000 | bytes 157286400 | tf_op jit(solution)/shard_map/ffn1/pallas_call | solution.py:107
  206.2 0.0 all-to-all-done.1
  206.3 0.0 copy-start.7
  206.3 0.0 copy-start.6
  206.3 5.1 %all-to-all-start.3 = ((bf16[8,40,4096]{2,1,0:T(8,128)(2,1)}), bf16[8,40,4096]{2,1,0:T(8,128)(2,1)}, u32[]{:S(2)}, u32[]{:S(2)}) async-start(bf16[8,40,4096]{2,1,0:T(8,128)(2,1)} %bitcast.27), calls=%async_computation.3 | async-start | bytes 5242880 | tf_op jit(solution)/shard_map/all_to_all | solution.py:152
  211.5 0.3 fusion.5
  211.7 5.0 %fusion.7 = f32[256,4096]{1,0:T(8,128)} fusion(bf16[256,320]{0,1:T(8,128)(2,1)S(1)} %get-tuple-element.6, bf16[320,4096]{1,0:T(8,128)(2,1)} %bitcast.6), kind=kOutput, calls=%fused_computation.20 | convolution fusion | flops 671088640 | bytes 6979584 | tf_op jit(solution)/shard_map/dot_general | solution.py:155
  216.7 54.8 %all-to-all-done.3 = bf16[8,40,4096]{2,1,0:T(8,128)(2,1)} async-done(((bf16[8,40,4096]{2,1,0:T(8,128)(2,1)}), bf16[8,40,4096]{2,1,0:T(8,128)(2,1)}, u32[]{:S(2)}, u32[]{:S(2)}) %all-to-all-start.3) | async-done | bytes 2621472 | tf_op jit(solution)/shard_map/all_to_all | solution.py:152
  271.5 5.6 %fusion.1 = bf16[1,1,256,4096]{3,2,1,0:T(8,128)(2,1)} fusion(f32[256,4096]{1,0:T(8,128)} %fusion.7, bf16[256,320]{0,1:T(8,128)(2,1)S(1)} %get-tuple-element.5, bf16[320,4096]{1,0:T(8,128)(2,1)} %bitcast.10), kind=kOutput, calls=%fused_computation.4 | convolution fusion | flops 673185792 | bytes 9076736 | tf_op jit(solution)/shard_map/dot_general | solution.py:155
  (16 shorter events, 0.0 us)
Async XLA Ops:
  0.0 2.0 copy-start
  0.2 4.2 %copy-start.1 = (s32[320]{0:T(512)}, s32[320]{0:T(512)S(1)}, u32[]{:S(2)}) copy-start(s32[320]{0:T(512)S(1)} %add.113) | copy-start | bytes 3844
  0.3 4.0 %copy-start.3 = (s32[320]{0:T(512)}, s32[320]{0:T(512)S(1)}, u32[]{:S(2)}) copy-start(s32[320]{0:T(512)S(1)} %add.107) | copy-start | bytes 3844
  1.2 0.6 copy-start.5
  4.4 66.5 %all-to-all-start = ((bf16[8,40,4096]{2,1,0:T(8,128)(2,1)}), bf16[8,40,4096]{2,1,0:T(8,128)(2,1)}, u32[]{:S(2)}, u32[]{:S(2)}) async-start(bf16[8,40,4096]{2,1,0:T(8,128)(2,1)} %bitcast.26), calls=%async_computation | async-start | bytes 5242880 | tf_op jit(solution)/shard_map/all_to_all | solution.py:147
  70.9 67.4 %all-to-all-start.2 = ((bf16[8,40,4096]{2,1,0:T(8,128)(2,1)}), bf16[8,40,4096]{2,1,0:T(8,128)(2,1)}, u32[]{:S(2)}, u32[]{:S(2)}) async-start(bf16[8,40,4096]{2,1,0:T(8,128)(2,1)} %bitcast.25), calls=%async_computation.2 | async-start | bytes 5242880 | tf_op jit(solution)/shard_map/all_to_all | solution.py:147
  138.2 68.0 %all-to-all-start.1 = ((bf16[8,40,4096]{2,1,0:T(8,128)(2,1)}), bf16[8,40,4096]{2,1,0:T(8,128)(2,1)}, u32[]{:S(2)}, u32[]{:S(2)}) async-start(bf16[8,40,4096]{2,1,0:T(8,128)(2,1)} %bitcast.28), calls=%async_computation.1 | async-start | bytes 5242880 | tf_op jit(solution)/shard_map/all_to_all | solution.py:152
  206.3 5.2 %copy-start.7 = (f32[1,1,256,2]{2,3,1,0:T(2,128)S(1)}, f32[1,1,256,2]{2,3,1,0:T(2,128)}, u32[]{:S(2)}) copy-start(f32[1,1,256,2]{2,3,1,0:T(2,128)} %param.10) | copy-start | bytes 6148
  206.3 5.2 %copy-start.2 = (s32[320]{0:T(512)S(1)}, s32[320]{0:T(512)}, u32[]{:S(2)}) copy-start(s32[320]{0:T(512)} %copy-done.1) | copy-start | bytes 3844
  206.3 5.2 %copy-start.4 = (s32[320]{0:T(512)S(1)}, s32[320]{0:T(512)}, u32[]{:S(2)}) copy-start(s32[320]{0:T(512)} %copy-done.3) | copy-start | bytes 3844
  206.3 5.2 %copy-start.6 = (s32[256,2]{0,1:T(2,128)S(1)}, s32[256,2]{0,1:T(2,128)}, u32[]{:S(2)}) copy-start(s32[256,2]{0,1:T(2,128)} %copy-done.5) | copy-start | bytes 6148
  206.3 65.2 %all-to-all-start.3 = ((bf16[8,40,4096]{2,1,0:T(8,128)(2,1)}), bf16[8,40,4096]{2,1,0:T(8,128)(2,1)}, u32[]{:S(2)}, u32[]{:S(2)}) async-start(bf16[8,40,4096]{2,1,0:T(8,128)(2,1)} %bitcast.27), calls=%async_computation.3 | async-start | bytes 5242880 | tf_op jit(solution)/shard_map/all_to_all | solution.py:152
